TPU v7x, 32 devices: a 4x4x1 block of a 4x4x8 slice. The times are simulated.
32 devices in a mesh: dp: 2 (over z, core), tp: 16 (over x, y).
Axes of the slice: x: 4, y: 4, z: 1, core: 2. Of those that a mesh axis runs over, the one named last changes fastest.
The devices are a block of a 4x4x8 slice.
Arguments:
- x: bfloat16 [8192, 4096], P(('dp', 'tp')), parts along dimension 0
- w_gate: bfloat16 [4096, 16384], P(None, 'tp')
- w_up: bfloat16 [4096, 16384], P(None, 'tp')
- w_down: bfloat16 [16384, 4096], P('tp')
Outputs:
- output: bfloat16 [8192, 4096], P(('dp', 'tp')), parts along dimension 0
There are 2 independent parts. A program takes and returns all parts, laid end to end along the dimension named above; an argument that names none is the same for every part.
All inputs are finite; a program needn't handle non-finite values.
Results may differ from a plain program's by a relative error of at most 0.016.
Values are sent between devices in bfloat16 or wider.
A program may use at most 768 MiB of HBM per device.

v0:
```python
import jax
import jax.numpy as jnp
from jax import lax
from jax.sharding import PartitionSpec as P


def solution(mesh):
    def step(x, w_gate, w_up, w_down):
        rows = lax.all_gather(x, "tp", axis=0, tiled=True)
        gate = jnp.dot(rows, w_gate, preferred_element_type=jnp.float32)
        up = jnp.dot(rows, w_up, preferred_element_type=jnp.float32)
        hidden = (jax.nn.silu(gate) * up).astype(jnp.bfloat16)
        term = jnp.dot(hidden, w_down, preferred_element_type=jnp.float32).astype(jnp.bfloat16)
        return lax.psum_scatter(term, "tp", scatter_dimension=0, tiled=True)

    return jax.shard_map(
        step,
        mesh=mesh,
        in_specs=(P(("dp", "tp"), None), P(None, "tp"), P(None, "tp"), P("tp", None)),
        out_specs=P(("dp", "tp"), None),
        check_vma=False,
    )
```

profile of v0, /device:TPU:97, one launch (start us, length us, event | category | flops | bytes accessed | tf_op | source)
XLA Modules:
  0.0 528.4 jit_solution(17740505036378140003)
XLA Ops:
  6.5 0.0 all-gather.2.cloned.1.call-start
  6.6 0.7 all-gather.2.cloned.1.call-update
  7.3 0.1 reduce-scatter.2.cloned.1.call-start
  7.4 197.4 %all-gather.2.cloned.1.call-done = bf16[4096,4096]{1,0:T(8,128)(2,1)} async-done(((bf16[256,4096]{1,0:T(8,128)(2,1)}), bf16[4096,4096]{1,0:T(8,128)(2,1)}) %all-gather.2.cloned.1.call-update) | async-done | bytes 33554448 | tf_op jit(solution)/shard_map/all_gather | solution.py:9
  204.8 41.0 %fusion.1 = f32[4096,1024]{1,0:T(8,128)S(1)} fusion(bf16[4096,4096]{1,0:T(8,128)(2,1)} %all-gather.2.cloned.1.call-done, bf16[4096,1024]{1,0:T(8,128)(2,1)} %param.5), kind=kOutput, calls=%fused_computation.3 | convolution fusion | flops 34359738368 | bytes 58720256 | tf_op jit(solution)/shard_map/dot_general | solution.py:10
  245.8 43.5 %multiply_convert_fusion.clone.4 = bf16[4096,1024]{1,0:T(8,128)(2,1)} fusion(f32[4096,1024]{1,0:T(8,128)S(1)} %fusion.1, bf16[4096,4096]{1,0:T(8,128)(2,1)} %all-gather.2.cloned.1.call-done, bf16[4096,1024]{1,0:T(8,128)(2,1)} %param.6), kind=kOutput, calls=%fused_computation.1.clone.clone.clone.1 | convolution fusion | flops 34384904192 | bytes 67108864 | tf_op jit(solution)/shard_map/dot_general | solution.py:11
  289.3 42.9 %convolution_convert_fusion = bf16[4096,4096]{1,0:T(8,128)(2,1)} fusion(bf16[1024,4096]{1,0:T(8,128)(2,1)} %param.7, bf16[4096,1024]{1,0:T(8,128)(2,1)} %multiply_convert_fusion.clone.4), kind=kOutput, calls=%fused_computation | convolution fusion | flops 34376515584 | bytes 50331648 | tf_op jit(solution)/shard_map/dot_general | solution.py:13
  332.2 0.1 reduce-scatter.2.cloned.1.call-update
  332.3 189.3 %reduce-scatter.2.cloned.1.call-done = bf16[256,4096]{1,0:T(8,128)(2,1)} async-done(((bf16[4096,4096]{1,0:T(8,128)(2,1)}), bf16[256,4096]{1,0:T(8,128)(2,1)}) %reduce-scatter.2.cloned.1.call-update) | async-done | bytes 2097168 | tf_op jit(solution)/shard_map/reduce_scatter | solution.py:14
Async XLA Ops:
  6.5 198.3 %all-gather.2.cloned.1.call-start = ((), (), s32[]{:S(2)}) async-start(), calls=%async_computation.1 | async-start | bytes 35651584 | tf_op jit(solution)/shard_map/all_gather | solution.py:9
  7.3 514.3 %reduce-scatter.2.cloned.1.call-start = ((), (), s32[]{:S(2)}) async-start(), calls=%async_computation.2 | async-start | bytes 35651584 | tf_op jit(solution)/shard_map/reduce_scatter | solution.py:14
Sparse Core Ops, SparseCore 0:
  9.3 195.4 all-gather.1
  332.4 189.1 reduce-scatter.1
where the time goes:
time: 529 us; the launch traced here: 528 us
  waiting for transfers between devices  388 us (73%)
  matrix products  127 us (24%)
  between operations  13.4 us (3%)
    all_gather x1, waiting for transfers between devices, step(): rows = lax.all_gather(x, 'tp', axis=0, tiled=True)  197 us
    reduce_scatter x1, waiting for transfers between devices, step(): return lax.psum_scatter(term, 'tp', scatter_dimension=0, tiled=True)  189 us
    dot_general x1, matrix products, step(): up = jnp.dot(rows, w_up, preferred_element_type=jnp.float32)  43.5 us
    dot_general x1, matrix products, step(): jnp.dot(hidden, w_down, preferred_element_type=jnp.float32)  42.9 us
    dot_general x1, matrix products, step(): gate = jnp.dot(rows, w_gate, preferred_element_type=jnp.float32)  41 us
  transfers between devices with their start and end apart: 2, of which 2 were waited for; matrix products, arithmetic and copies ran while one was open for 0% of the time, Pallas kernels for 0%

commit v1 on v0

v1 whole, which is shorter than its diff:
```python
import functools
import math

import jax
import jax.numpy as jnp
from jax import lax
from jax.experimental import pallas as pl
from jax.experimental.pallas import tpu as pltpu
from jax.sharding import PartitionSpec as P

MESH = pl.DeviceIdType.MESH
RINGS = 4
HALVES = 2
TILE_F = 256
TILE_D = 512


def neighbours(n):
    side = math.isqrt(n)
    me = lax.axis_index("tp")
    x, y = me // side, lax.rem(me, side)
    k = lax.rem(x + y, side)

    def first(p):
        row = p // side
        return lax.rem(lax.rem(p, side) - row + side, side) * side + row

    def second(p):
        col = p // side
        return col * side + lax.rem(lax.rem(p, side) - col + side, side)

    p1, p2 = y * side + k, x * side + k
    return (
        first(lax.rem(p1 + 1, n)),
        first(lax.rem(p1 + n - 1, n)),
        second(lax.rem(p2 + 1, n)),
        second(lax.rem(p2 + n - 1, n)),
    )


def kernel(n, x_ref, wg_ref, wu_ref, wd_ref, out_ref, xbuf, wg, wu, wd, xv, hidden, yin, yout,
           w_sem, l_sem, o_sem, xs_sem, xr_sem, ys_sem, yr_sem):
    rows, d = x_ref.shape
    ff = wg.shape[1]
    part = rows // RINGS
    half = d // HALVES
    nxt = neighbours(n)

    loads = [pltpu.make_async_copy(a, b, w_sem.at[i])
             for i, (a, b) in enumerate(((wg_ref, wg), (wu_ref, wu), (wd_ref, wd)))]
    for c in loads:
        c.start()
    yin[1] = jnp.zeros(yin.shape[1:], yin.dtype)

    barrier = pltpu.get_barrier_semaphore()
    for r in range(RINGS):
        pl.semaphore_signal(barrier, inc=1, device_id={"tp": nxt[r]}, device_id_type=MESH)
    pl.semaphore_wait(barrier, RINGS)

    def x_copy(s, r, src):
        return pltpu.make_async_remote_copy(
            src_ref=src, dst_ref=xbuf.at[s, r], send_sem=xs_sem.at[s, r], recv_sem=xr_sem.at[s, r],
            device_id={"tp": nxt[r]}, device_id_type=MESH)

    def y_copy(src_slot, dst_slot, h, r):
        band = pl.ds(r * part, part)
        return pltpu.make_async_remote_copy(
            src_ref=yout.at[src_slot, h, band], dst_ref=yin.at[dst_slot, h, band],
            send_sem=ys_sem.at[src_slot, h, r], recv_sem=yr_sem.at[dst_slot, h, r],
            device_id={"tp": nxt[r]}, device_id_type=MESH)

    for r in range(RINGS):
        x_copy(0, r, x_ref.at[pl.ds(r * part, part)]).start()
    for c in loads:
        c.wait()

    def step(s, carry):
        slot, other = lax.rem(s, 2), lax.rem(s + 1, 2)

        @pl.when(s < n)
        def _():
            for r in range(RINGS):
                x_copy(s - 1, r, xbuf.at[s - 1, r]).wait_recv()

                @pl.when(s < n - 1)
                def _():
                    x_copy(s, r, xbuf.at[s - 1, r]).start()

                pltpu.make_async_copy(xbuf.at[s - 1, r], xv.at[pl.ds(r * part, part)], l_sem.at[r]).start()

        @pl.when(s == n)
        def _():
            for r in range(RINGS):
                band = pl.ds(r * part, part)
                pltpu.make_async_copy(x_ref.at[band], xv.at[band], l_sem.at[r]).start()

        for r in range(RINGS):
            band = pl.ds(r * part, part)
            pltpu.make_async_copy(x_ref.at[band], xv.at[band], l_sem.at[r]).wait()

        @pl.loop(0, ff // TILE_F)
        def _(j):
            cols = pl.ds(pl.multiple_of(j * TILE_F, TILE_F), TILE_F)
            gate = jnp.dot(xv[...], wg[:, cols], preferred_element_type=jnp.float32)
            up = jnp.dot(xv[...], wu[:, cols], preferred_element_type=jnp.float32)
            hidden[:, cols] = (jax.nn.silu(gate) * up).astype(hidden.dtype)

        for h in range(HALVES):
            @pl.when(s >= 3)
            def _():
                for r in range(RINGS):
                    y_copy(slot, other, h, r).wait_send()

            @pl.when(s >= 2)
            def _():
                for r in range(RINGS):
                    y_copy(other, slot, h, r).wait_recv()

            @pl.loop(0, half // TILE_D)
            def _(j):
                cols = pl.ds(pl.multiple_of(j * TILE_D, TILE_D), TILE_D)
                wcols = pl.ds(pl.multiple_of(h * half + j * TILE_D, TILE_D), TILE_D)
                term = jnp.dot(hidden[...], wd[:, wcols], preferred_element_type=jnp.float32)
                total = term + yin[slot, h, :, cols].astype(jnp.float32)
                yout[slot, h, :, cols] = total.astype(yout.dtype)

            @pl.when(s < n)
            def _():
                for r in range(RINGS):
                    y_copy(slot, other, h, r).start()

            @pl.when(s == n)
            def _():
                pltpu.make_async_copy(yout.at[slot, h], out_ref.at[:, pl.ds(h * half, half)], o_sem.at[h]).start()

        return carry

    lax.fori_loop(1, n + 1, step, 0)

    for h in range(HALVES):
        pltpu.make_async_copy(yout.at[n % 2, h], out_ref.at[:, pl.ds(h * half, half)], o_sem.at[h]).wait()
        for r in range(RINGS):
            y_copy((n - 1) % 2, n % 2, h, r).wait_send()

    def drain(s, carry):
        for r in range(RINGS):
            x_copy(s, r, xbuf.at[s, r]).wait_send()
        return carry

    lax.fori_loop(0, n - 1, drain, 0)


def solution(mesh):
    n = mesh.shape["tp"]

    def step(x, w_gate, w_up, w_down):
        rows, d = x.shape
        ff = w_gate.shape[1]
        part, half = rows // RINGS, d // HALVES
        dt = x.dtype
        y, _ = pl.pallas_call(
            functools.partial(kernel, n),
            out_shape=(jax.ShapeDtypeStruct((rows, d), dt),
                       jax.ShapeDtypeStruct((n - 1, RINGS, part, d), dt)),
            in_specs=[pl.BlockSpec(memory_space=pltpu.HBM)] * 4,
            out_specs=[pl.BlockSpec(memory_space=pltpu.HBM)] * 2,
            scratch_shapes=[
                pltpu.VMEM((d, ff), dt),
                pltpu.VMEM((d, ff), dt),
                pltpu.VMEM((ff, d), dt),
                pltpu.VMEM((rows, d), dt),
                pltpu.VMEM((rows, ff), dt),
                pltpu.VMEM((2, HALVES, rows, half), dt),
                pltpu.VMEM((2, HALVES, rows, half), dt),
                pltpu.SemaphoreType.DMA((3,)),
                pltpu.SemaphoreType.DMA((RINGS,)),
                pltpu.SemaphoreType.DMA((HALVES,)),
                pltpu.SemaphoreType.DMA((n - 1, RINGS)),
                pltpu.SemaphoreType.DMA((n - 1, RINGS)),
                pltpu.SemaphoreType.DMA((2, HALVES, RINGS)),
                pltpu.SemaphoreType.DMA((2, HALVES, RINGS)),
            ],
            compiler_params=pltpu.CompilerParams(
                collective_id=0, has_side_effects=True, vmem_limit_bytes=60 * 2**20),
        )(x, w_gate, w_up, w_down)
        return y

    return jax.shard_map(
        step,
        mesh=mesh,
        in_specs=(P(("dp", "tp"), None), P(None, "tp"), P(None, "tp"), P("tp", None)),
        out_specs=P(("dp", "tp"), None),
        check_vma=False,
    )
```

time: 529 us -> 355 us (0.67)
  waiting for transfers between devices: 388 us -> 0 us
  Pallas kernels: 0 us -> 350 us
  matrix products: 127 us -> 0 us
  between operations: 13.4 us -> 0.01 us
    pallas_call x0 -> x1, Pallas kernels: none -> 350 us  [step(): pl.pallas_call(functools.partial(kernel, n), out_shape=(jax.ShapeDtypeStr...]
    all_gather x1 -> x0, waiting for transfers between devices: 197 us -> none  [step(): rows = lax.all_gather(x, 'tp', axis=0, tiled=True)]
    reduce_scatter x1 -> x0, waiting for transfers between devices: 189 us -> none  [step(): return lax.psum_scatter(term, 'tp', scatter_dimension=0, tiled=True)]
    dot_general x3 -> x0, matrix products: 127 us -> none  [the longest x1 43.5 us: step(): up = jnp.dot(rows, w_up, preferred_element_type=jnp.float32)]
  transfers between devices with their start and end apart: 2 -> 0, of which waited for: 2 -> 0; matrix products, arithmetic and copies ran while one was open for 0% -> 0% of each run, Pallas kernels for 0% -> 0%
where the time goes in v1:
time: 355 us; the launch traced here: 353 us
  Pallas kernels  350 us (99%)
    pallas_call x1, Pallas kernels, step(): pl.pallas_call(functools.partial(kernel, n), out_shape=(jax.ShapeDtypeStr...  350 us

profile of v1, /device:TPU:97, one launch (start us, length us, event | category | flops | bytes accessed | tf_op | source)
XLA Modules:
  0.0 353.0 jit_solution(8353790042971513658)
XLA Ops:
  0.0 349.8 %shard_map.46 = (bf16[256,4096]{1,0:T(8,128)(2,1)}, bf16[15,4,64,4096]{3,2,1,0:T(8,128)(2,1)}) custom-call(bf16[256,4096]{1,0:T(8,128)(2,1)} %x_ref.1, bf16[4096,1024]{1,0:T(8,128)(2,1)} %wg_ref.1, bf16[4096,1024]{1,0:T(8,128)(2,1)} %wu_ref.1, bf16[1024,4096]{1,0:T(8,128)(2,1)} %wd_ref.1), custom_call_target="tpu_custom_call" | custom-call | tf_op jit(solution)/shard_map/pallas_call | solution.py:161
  349.8 3.1 copy.6

commit v2 on v0

v2 whole, which is shorter than its diff:
```python
import functools
import math

import jax
import jax.numpy as jnp
from jax import lax
from jax.experimental import pallas as pl
from jax.experimental.pallas import tpu as pltpu
from jax.sharding import PartitionSpec as P

MESH = pl.DeviceIdType.MESH
ZROWS = 48
PIECES = 4
TILE_F = 512
TILE_D = 256


def kernel(n, x_ref, wg_ref, wu_ref, wd_ref, out_ref, xg, wdx,
           wg, wu, wgx, wux, xv, hid, hs, yin, yout, wt, rel,
           own_sem, stage_sem, wt_sem, out_sem, xs, xr, ws, wr, ds, dr, ys, yr, rs, rr):
    side = math.isqrt(n)
    ring = n // 2
    rows, d = x_ref.shape
    ff = wg.shape[1]
    half, quarter, width = rows // 2, ff // 4, d // PIECES
    srows = half - 2 * ZROWS
    tiles = width // TILE_D

    me, dp = lax.axis_index("tp"), lax.axis_index("dp")
    x, y = me // side, lax.rem(me, side)
    u = lax.rem(x - y + side, side)
    k, v = u // 2, lax.rem(u, 2)
    q = 2 * y + v
    m = lax.rem(q, 4)
    core = lax.rem(dp, 2)
    partner = dp + 1 - 2 * core

    def wrap(p):
        return lax.rem(p + 2 * ring, ring)

    def device(p):
        row = p // 2
        return lax.rem(row + 2 * k + lax.rem(p, 2), side) * side + row

    sp, sm = device(wrap(q + 1)), device(wrap(q - 1))
    cross = (lax.rem(x + 2 * v - 1 + side, side) * side + y, x * side + lax.rem(y + 1 - 2 * v + side, side))
    cp = cross[1] + v * (cross[0] - cross[1])
    cm = cross[0] + v * (cross[1] - cross[0])

    def remote(src, dst, send, recv, tp=None):
        device_id = {"dp": partner} if tp is None else {"tp": tp}
        return pltpu.make_async_remote_copy(
            src_ref=src, dst_ref=dst, send_sem=send, recv_sem=recv, device_id=device_id, device_id_type=MESH)

    def chunk(way, j):
        t = j // 2 + 1
        return (wrap(q - t), j % 2) if way == 0 else (wrap(q + t), 1 - j % 2)

    def hband(h):
        return pl.ds(h * half, half)

    def x_send(way, j):
        t = j // 2 + 1
        owner, h = (wrap(q - t + 1), j % 2) if way == 0 else (wrap(q + t - 1), 1 - j % 2)
        src = x_ref.at[hband(h)] if t == 1 else xg.at[owner, hband(h)]
        return remote(src, xg.at[owner, hband(h)], xs.at[j, way], xr.at[j, way], (sp, sm)[way])

    last = ring - 2

    def w_views(piece, index):
        if piece == 2:
            band = pl.ds(pl.multiple_of(index * quarter, quarter), quarter)
            return wd_ref.at[band], wdx.at[band]
        cols = pl.ds(pl.multiple_of(index * quarter, quarter), quarter)
        return (wg_ref, wu_ref)[piece].at[:, cols], (wgx, wux)[piece].at[:, cols]

    def w_send(piece, link):
        src, dst = w_views(piece, 2 * link + core)
        return remote(src, dst, ws.at[piece, link], wr.at[piece, link], cross[link])

    def w_share(piece, link):
        _, dst = w_views(piece, 2 * link + core)
        return remote(dst, dst, ds.at[piece, link], dr.at[piece, link])

    def pass_on(piece):
        for link in range(2):
            w_send(piece, link).wait_recv()
            w_share(piece, link).start()

    loads = [pltpu.make_async_copy(a, b, own_sem.at[i]) for i, (a, b) in enumerate(((wg_ref, wg), (wu_ref, wu)))]
    for c in loads:
        c.start()
    yin[1] = jnp.zeros(yin.shape[1:], yin.dtype)
    barrier = pltpu.get_barrier_semaphore()
    for tp in (sp, sm, cp, cm):
        pl.semaphore_signal(barrier, inc=1, device_id={"tp": tp}, device_id_type=MESH)
    pl.semaphore_signal(barrier, inc=1, device_id={"dp": partner}, device_id_type=MESH)
    pl.semaphore_wait(barrier, 5)
    for j in range(2):
        for way in range(2):
            x_send(way, j).start()
    for piece in range(3):
        for link in range(2):
            w_send(piece, link).start()

    def blocks(unit):
        if unit == 0:
            return (q, 0), (q, 1)
        return chunk(0, unit - 1), chunk(1, unit - 1)

    def stage(unit, slot):
        out = []
        for i, (owner, h) in enumerate(blocks(unit)):
            src = x_ref.at[hband(h)] if unit == 0 else xg.at[owner, hband(h)]
            out.append(pltpu.make_async_copy(src, xv.at[slot, hband(i)], stage_sem.at[slot, i]))
        return out

    def start(copies):
        for c in copies:
            c.start()

    def wait(copies):
        for c in copies:
            c.wait()

    def work(unit, slot, other):
        gates, ups = (wgx, wux) if other else (wg, wu)
        (o0, h0), (o1, h1) = blocks(unit)
        base = ff if other else 0

        @pl.loop(0, ff // TILE_F)
        def _(j):
            cols = pl.ds(pl.multiple_of(j * TILE_F, TILE_F), TILE_F)
            to = pl.ds(pl.multiple_of(base + j * TILE_F, TILE_F), TILE_F)
            gate = jnp.dot(xv[slot], gates[:, cols], preferred_element_type=jnp.float32)
            up = jnp.dot(xv[slot], ups[:, cols], preferred_element_type=jnp.float32)
            act = (jax.nn.silu(gate) * up).astype(hid.dtype)
            hid[o0, hband(h0), to] = act[:half]
            hid[o1, hband(h1), to] = act[half:]

    def arrive(j):
        for way in range(2):
            x_send(way, j).wait_recv()
            if j + 2 <= last:
                x_send(way, j + 2).start()

    def run(jobs):
        start(stage(jobs[0][0], 0))
        for i, (unit, other) in enumerate(jobs):
            wait(stage(unit, i % 2))
            if i + 1 < len(jobs):
                start(stage(jobs[i + 1][0], (i + 1) % 2))
            work(unit, i % 2, other)

    start(stage(0, 0))
    wait(loads)
    wait(stage(0, 0))
    work(0, 0, False)
    for j in range(2):
        arrive(j)
        run([(j + 1, False)])
    arrive(2)
    run([(3, False)])
    pass_on(0)
    arrive(3)
    start(stage(4, 0))
    wait(stage(4, 0))
    work(4, 0, False)
    pass_on(1)
    for piece in range(2):
        for link in range(2):
            w_share(piece, link).wait_recv()
    run([(0, True), (1, True)])
    arrive(4)
    run([(5, False), (2, True), (3, True)])
    arrive(5)
    run([(6, False)])
    pass_on(2)
    run([(4, True)])
    for link in range(2):
        w_share(2, link).wait_recv()

    offs = (0, srows, srows + ZROWS, half, half + srows, half + srows + ZROWS)
    sizes = (srows, ZROWS, ZROWS) * 2

    def fold(p):
        f = lax.rem(p, 4)
        return p + (f // 2) * (5 - 2 * f)

    def owner(r, s):
        if r == 0:
            return wrap(q - s)
        if r == 3:
            return wrap(q + s)
        shift = (0, 0, 2, 0, 1, 3)[r]
        p = fold(wrap(q - shift))
        return wrap(fold(wrap(p - s if r < 3 else p + s)) + shift)

    in12, in23 = lax.rem((m + 1) // 2, 2), m // 2

    def zband(way, index):
        return pl.ds(pl.multiple_of(way * half + srows + index * ZROWS, 8), ZROWS)

    def y_sends(slot, c):
        to = 1 - slot
        out = [remote(yout.at[slot, c, pl.ds(offs[r], sizes[r])], yin.at[to, c, pl.ds(offs[r], sizes[r])],
                      ys.at[slot, c, way], yr.at[to, c, r], (sp, sm)[way]) for way, r in ((0, 0), (1, 3))]
        for way, index, tp in ((0, in12, sp + v * (sm - sp)), (1, 1 - in23, sm + v * (sp - sm))):
            band = zband(way, index)
            out.append(remote(yout.at[slot, c, band], yin.at[to, c, band], ys.at[slot, c, 2 + way],
                              yr.at[to, c, 3 * way + 1 + index], tp))
        for way, index, tp in ((0, 1 - in12, cp), (1, in23, cm)):
            out.append(remote(yout.at[slot, c, zband(way, index)], rel.at[way, slot, c], ys.at[slot, c, 4 + way],
                              rr.at[way, slot, c], tp))
        return out

    def relays(slot, c):
        to = 1 - slot
        return [remote(rel.at[way, slot, c], yin.at[to, c, zband(way, index)], rs.at[way, slot, c],
                       yr.at[to, c, 3 * way + 1 + index], tp)
                for way, index, tp in ((0, in23, cp), (1, 1 - in12, cm))]

    def relay(slot, c):
        for way, copy in enumerate(relays(slot, c)):
            landed = rel.at[way, slot, c]
            remote(landed, landed, rs.at[way, slot, c], rr.at[way, slot, c], cp).wait_recv()
            copy.start()

    def y_waits(slot, c):
        for r in range(6):
            band = pl.ds(offs[r], sizes[r])
            remote(yin.at[slot, c, band], yin.at[slot, c, band], ys.at[slot, c, 0], yr.at[slot, c, r], sp).wait_recv()

    def w_tile(index, slot):
        cols = pl.ds(pl.multiple_of(index * TILE_D, TILE_D), TILE_D)
        return [pltpu.make_async_copy(ref.at[:, cols], wt.at[slot, pl.ds(i * ff, ff)], wt_sem.at[slot, i])
                for i, ref in enumerate((wd_ref, wdx))]

    ahead = tiles - 1
    for i in range(ahead):
        start(w_tile(i, i))

    def out_copy(slot, c):
        return pltpu.make_async_copy(yout.at[slot, c], out_ref.at[:, pl.ds(c * width, width)], out_sem.at[c])

    def step(s, carry):
        slot = lax.rem(s, 2)
        for r in range(6):
            band = pl.ds(offs[r], sizes[r])
            hs[band] = hid[owner(r, s), band]

        for c in range(PIECES):
            @pl.when(s >= 3)
            def _():
                for copy in y_sends(slot, c):
                    copy.wait_send()

            @pl.when(s >= 2)
            def _():
                y_waits(slot, c)

            @pl.loop(0, tiles)
            def _(i):
                wait(w_tile(0, i))

                @pl.when((s < ring) | (c * tiles + i + ahead < PIECES * tiles))
                def _():
                    start(w_tile(lax.rem(c * tiles + i + ahead, PIECES * tiles), lax.rem(i + ahead, tiles)))

                cols = pl.ds(pl.multiple_of(i * TILE_D, TILE_D), TILE_D)
                term = jnp.dot(hs[...], wt[i], preferred_element_type=jnp.float32)
                total = term + yin[slot, c, :, cols].astype(jnp.float32)
                yout[slot, c, :, cols] = total.astype(yout.dtype)

            @pl.when(s >= 2)
            def _():
                for copy in relays(1 - slot, c):
                    copy.wait_send()

            @pl.when(s < ring)
            def _():
                start(y_sends(slot, c))
                if c:
                    relay(slot, c - 1)

            @pl.when(s == ring)
            def _():
                out_copy(slot, c).start()

        @pl.when(s == 1)
        def _():
            run([(5, True)])

        @pl.when(s == 2)
        def _():
            arrive(last)
            run([(last + 1, False)])

        @pl.when(s < ring)
        def _():
            relay(slot, PIECES - 1)

        @pl.when(s == 1)
        def _():
            run([(6, True)])

        @pl.when(s == 2)
        def _():
            run([(last + 1, True)])

        return carry

    lax.fori_loop(1, ring + 1, step, 0)

    for c in range(PIECES):
        for copy in y_sends((ring - 1) % 2, c):
            copy.wait_send()
        out_copy(ring % 2, c).wait()
    for way in range(2):
        for j in range(last + 1):
            x_send(way, j).wait_send()
    for piece in range(3):
        for link in range(2):
            w_send(piece, link).wait_send()
            w_share(piece, link).wait_send()


def solution(mesh):
    n = mesh.shape["tp"]
    ring = n // 2

    def step(x, w_gate, w_up, w_down):
        rows, d = x.shape
        ff = w_gate.shape[1]
        dt = x.dtype
        width = d // PIECES
        dma = pltpu.SemaphoreType.DMA
        y, _, _ = pl.pallas_call(
            functools.partial(kernel, n),
            out_shape=(jax.ShapeDtypeStruct((rows, d), dt),
                       jax.ShapeDtypeStruct((ring, rows, d), dt),
                       jax.ShapeDtypeStruct((ff, d), dt)),
            in_specs=[pl.BlockSpec(memory_space=pltpu.HBM)] * 4,
            out_specs=[pl.BlockSpec(memory_space=pltpu.HBM)] * 3,
            scratch_shapes=[
                pltpu.VMEM((d, ff), dt),
                pltpu.VMEM((d, ff), dt),
                pltpu.VMEM((d, ff), dt),
                pltpu.VMEM((d, ff), dt),
                pltpu.VMEM((2, rows, d), dt),
                pltpu.VMEM((ring, rows, 2 * ff), dt),
                pltpu.VMEM((rows, 2 * ff), dt),
                pltpu.VMEM((2, PIECES, rows, width), dt),
                pltpu.VMEM((2, PIECES, rows, width), dt),
                pltpu.VMEM((width // TILE_D, 2 * ff, TILE_D), dt),
                pltpu.VMEM((2, 2, PIECES, ZROWS, width), dt),
                dma((2,)),
                dma((2, 2)),
                dma((width // TILE_D, 2)),
                dma((PIECES,)),
                dma((ring - 1, 2)),
                dma((ring - 1, 2)),
                dma((3, 2)),
                dma((3, 2)),
                dma((3, 2)),
                dma((3, 2)),
                dma((2, PIECES, 6)),
                dma((2, PIECES, 6)),
                dma((2, 2, PIECES)),
                dma((2, 2, PIECES)),
            ],
            compiler_params=pltpu.CompilerParams(
                collective_id=0, has_side_effects=True, vmem_limit_bytes=67_000_000),
        )(x, w_gate, w_up, w_down)
        return y

    return jax.shard_map(
        step,
        mesh=mesh,
        in_specs=(P(("dp", "tp"), None), P(None, "tp"), P(None, "tp"), P("tp", None)),
        out_specs=P(("dp", "tp"), None),
        check_vma=False,
    )
```

time: 529 us -> 313 us (0.59)
  waiting for transfers between devices: 388 us -> 0 us
  Pallas kernels: 0 us -> 305 us
  matrix products: 127 us -> 0 us
  between operations: 13.4 us -> 0.01 us
    pallas_call x0 -> x1, Pallas kernels: none -> 305 us  [step(): pl.pallas_call(functools.partial(kernel, n), out_shape=(jax.ShapeDtypeStr...]
    all_gather x1 -> x0, waiting for transfers between devices: 197 us -> none  [step(): rows = lax.all_gather(x, 'tp', axis=0, tiled=True)]
    reduce_scatter x1 -> x0, waiting for transfers between devices: 189 us -> none  [step(): return lax.psum_scatter(term, 'tp', scatter_dimension=0, tiled=True)]
    dot_general x3 -> x0, matrix products: 127 us -> none  [the longest x1 43.5 us: step(): up = jnp.dot(rows, w_up, preferred_element_type=jnp.float32)]
  transfers between devices with their start and end apart: 2 -> 0, of which waited for: 2 -> 0; matrix products, arithmetic and copies ran while one was open for 0% -> 0% of each run, Pallas kernels for 0% -> 0%
where the time goes in v2:
time: 313 us; the launch traced here: 308 us
  Pallas kernels  305 us (97%)
  local copies, waits for them, and re-layouts  3.13 us (1%)
    pallas_call x1, Pallas kernels, step(): pl.pallas_call(functools.partial(kernel, n), out_shape=(jax.ShapeDtypeStr...  305 us

profile of v2, /device:TPU:97, one launch (start us, length us, event | category | flops | bytes accessed | tf_op | source)
XLA Modules:
  0.0 307.7 jit_solution(3695412726299854473)
XLA Ops:
  0.0 304.6 %shard_map.46 = (bf16[256,4096]{1,0:T(8,128)(2,1)}, bf16[8,256,4096]{2,1,0:T(8,128)(2,1)}, bf16[1024,4096]{1,0:T(8,128)(2,1)}) custom-call(bf16[256,4096]{1,0:T(8,128)(2,1)} %x_ref.1, bf16[4096,1024]{1,0:T(8,128)(2,1)} %wg_ref.1, bf16[4096,1024]{1,0:T(8,128)(2,1)} %wu_ref.1, bf16[1024,4096]{1,0:T(8,128)(2,1)} %wd_ref.1), custom_call_target="tpu_custom_call" | custom-call | tf_op jit(solution)/shard_map/pallas_call | solution.py:338
  304.6 3.1 %copy.6 = bf16[256,4096]{1,0:T(8,128)(2,1)} copy(bf16[256,4096]{1,0:T(8,128)(2,1)} %get-tuple-element.6) | data formatting | bytes 4194304
